TPU v7x, 256 devices: a whole 4x4x8 slice. The times are simulated.
256 devices in a mesh: rep: 4 (over z_hi), exp: 8 (over x, core), shard: 8 (over z_lo, y).
Axes of the slice: x: 4, y: 4, z: 8 (z_hi: 4, z_lo: 2; z = z_hi * 2 + z_lo), core: 2. Of those that a mesh axis runs over, the one named last changes fastest.
Arguments:
- tokens: bfloat16 [28672, 2048], P(('rep', 'exp', 'shard')), may hold values from -1.5 to 1.5
- routes: int32 [28672, 2], P(('rep', 'exp', 'shard')), may hold values from 0 to 7, all different within a row; in each aligned block of 112 rows (0 to 111, 112 to 223, ...) at most 31 rows name the same one
- gate_weight: bfloat16 [8, 2048, 7168], P('exp', None, 'shard'), may hold values from -0.125 to 0.125
- gate_cotangent: bfloat16 [8, 7936, 7168], P('exp', 'rep', 'shard'), may hold values from -0.75 to 0.75
Outputs:
- token_grad: bfloat16 [28672, 2048], P(('rep', 'exp', 'shard'))
- weight_grad: bfloat16 [8, 2048, 7168], P('exp', None, 'shard')
Inputs may be any that keep to these rules, and one draw needn't show every extreme that they name: `routes`: the two entries of a row differ. The rows of one device name one expert at most 31 times, and some device names some expert exactly 31 times.
All inputs are finite; a program needn't handle non-finite values.
Results may differ from a plain program's by a relative error of at most 0.015.
Values may be sent and summed in bfloat16 or wider, within the bound.
A program may use at most 128 MiB of HBM per device.

v0:
```python
import jax
import jax.numpy as jnp
from jax import lax
from jax.sharding import PartitionSpec as P


def in_blocks(shard, dim, size):
    before, after = (shard.shape[:dim], shard.shape[dim + 1 :])
    return jnp.moveaxis(shard.reshape(*before, size, -1, *after), dim, 0)


def cut_rows(length, count):
    lap = length // count
    if lap >= 8:
        lap -= lap % 8
    return [lap * k for k in range(1, count)]


def laid_out(blocks, dim):
    lengths = list(blocks.shape[1:])
    lengths[dim] *= blocks.shape[0]
    return jnp.moveaxis(blocks, 0, dim).reshape(lengths)


def cut_exchange(shard, axis, pieces, split_dim, concat_dim):
    blocks = in_blocks(shard, split_dim, lax.axis_size(axis))
    cut = max(range(1, max(2, blocks.ndim - 1)), key=lambda d: blocks.shape[d])
    gathered = []
    for slab in jnp.split(blocks, cut_rows(blocks.shape[cut], pieces), axis=cut):
        if slab.size:
            gathered.append(lax.all_to_all(slab, axis, split_axis=0, concat_axis=0, tiled=True))
    return laid_out(jnp.concatenate(gathered, axis=cut), concat_dim)


def slot_matrix(route_rows, experts, slot_cap):
    expert_ids = jnp.arange(experts, dtype=jnp.int32)
    onehot = (route_rows[:, :, None] == expert_ids[None, None, :]).astype(jnp.int32)
    flattened = onehot.reshape(-1, experts)
    before = jnp.cumsum(flattened, axis=0) - flattened
    position = jnp.sum(before * flattened, axis=1)
    target = jnp.sum(flattened * expert_ids[None, :], axis=1) * slot_cap + position
    slot_ids = jnp.arange(experts * slot_cap, dtype=jnp.int32)
    matches = (target[None, :] == slot_ids[:, None]).astype(jnp.int32)
    return matches.reshape(experts * slot_cap, -1, 2).sum(axis=2)


def body(tokens, routes, gate_weight, gate_cotangent):
    experts = lax.axis_size("exp")
    shards = lax.axis_size("shard")
    features = tokens.shape[1]
    cotangent = gate_cotangent[0]
    hidden = cotangent.shape[1]
    slot_cap = cotangent.shape[0] // (experts * shards)
    weight = gate_weight[0]
    blocks = cotangent.reshape(experts, shards, slot_cap, hidden)
    placing = slot_matrix(routes, experts, slot_cap).astype(jnp.bfloat16)
    outgoing = jnp.dot(placing, tokens, preferred_element_type=jnp.float32).astype(jnp.bfloat16)
    outgoing = outgoing.reshape(experts, slot_cap, features)
    contract_rows = (((0,), (0,)), ((), ()))
    copies = jnp.broadcast_to(outgoing[:, None], (experts, shards, slot_cap, features))
    copies = copies.reshape(experts * shards, slot_cap, features)
    arrived = cut_exchange(copies, ("exp", "shard"), 2, 0, 0)
    partial_grad = lax.dot_general(
        arrived.reshape(-1, features), cotangent, contract_rows, preferred_element_type=jnp.float32
    )
    weight_grad = lax.psum(partial_grad.astype(jnp.bfloat16), "rep")[None]
    ordered = jnp.swapaxes(blocks, 0, 1).reshape(-1, hidden)
    summed = lax.psum_scatter(
        lax.dot_general(
            ordered, weight, (((1,), (1,)), ((), ())), preferred_element_type=jnp.float32
        ).astype(jnp.bfloat16),
        "shard",
        scatter_dimension=0,
        tiled=True,
    )
    slot_grad = summed.reshape(experts, slot_cap, features)
    returned = lax.all_to_all(slot_grad, "exp", split_axis=0, concat_axis=0, tiled=True)
    token_grad = jnp.dot(
        placing.T, returned.reshape(-1, features), preferred_element_type=jnp.float32
    )
    return (token_grad.astype(jnp.bfloat16), weight_grad)


def solution(mesh):
    placed = (
        P(("rep", "exp", "shard"), None),
        P(("rep", "exp", "shard"), None),
        P("exp", None, "shard"),
        P("exp", "rep", "shard"),
    )
    return jax.shard_map(
        body,
        mesh=mesh,
        in_specs=placed,
        out_specs=(P(("rep", "exp", "shard"), None), P("exp", None, "shard")),
        check_vma=False,
    )
```

profile of v0, /device:TPU:39, one launch (start us, length us, event | category | flops | bytes accessed | tf_op | source)
XLA Modules:
  0.0 382.8 jit_solution(11135066834994164026)
XLA Ops:
  8.0 0.0 copy-start
  8.0 0.8 copy.10
  8.8 0.1 eq.37
  9.0 0.6 reduce-window.6
  9.6 0.2 slice_reduce_fusion
  9.9 0.1 add_bitcast_fusion
  10.0 0.1 add.15
  10.1 0.1 copy.11
  10.2 0.1 convert_reduce_fusion
  10.3 0.0 copy-done
  10.3 0.4 convolution_convert_fusion.1
  10.8 0.3 broadcast_in_dim.6
  11.1 1.1 broadcast_in_dim.7
  12.1 0.0 copy-start.2
  12.2 3.2 copy-done.2
  15.4 1.4 split.8
  16.8 9.4 %all-to-all-start.1 = ((bf16[64,1,8,2048]{3,2,1,0:T(8,128)(2,1)}), bf16[64,1,8,2048]{3,2,1,0:T(8,128)(2,1)S(1)}, u32[]{:S(2)}, u32[]{:S(2)}) async-start(bf16[64,1,8,2048]{3,2,1,0:T(8,128)(2,1)} %split.8), calls=%async_computation.2 | async-start | bytes 4194304 | tf_op jit(solution)/shard_map/all_to_all | solution.py:31
  26.3 0.0 reduce-scatter.2.cloned.1.call-start
  26.3 4.8 %reshape_squeeze.3 = bf16[8,8,31,896]{3,2,1,0:T(8,128)(2,1)} reshape(bf16[1,1984,896]{2,1,0:T(8,128)(2,1)} %param.7) | data formatting | bytes 7110656 | tf_op jit(solution)/shard_map/reshape;squeeze | solution.py:55
  31.1 4.3 %copy.12 = bf16[8,8,31,896]{3,2,1,0:T(8,128)(2,1)} copy(bf16[8,8,31,896]{3,2,0,1:T(8,128)(2,1)} %bitcast.22) | data formatting | bytes 7110656 | tf_op jit(solution)/shard_map/transpose | solution.py:67
  35.4 4.8 %reshape.51 = bf16[1984,896]{1,0:T(8,128)(2,1)} reshape(bf16[8,8,31,896]{3,2,1,0:T(8,128)(2,1)} %copy.12) | data formatting | bytes 7110656 | tf_op jit(solution)/shard_map/reshape | solution.py:67
  40.2 13.4 %convolution_convert_fusion = bf16[1984,2048]{1,0:T(8,128)(2,1)} fusion(bf16[1984,896]{1,0:T(8,128)(2,1)} %reshape.51, bf16[1,2048,896]{2,1,0:T(8,128)(2,1)} %param.6), kind=kOutput, calls=%fused_computation.1 | convolution fusion | flops 7285374976 | bytes 15351808 | tf_op jit(solution)/shard_map/dot_general | solution.py:69
  53.6 0.0 reduce-scatter.2.cloned.1.call-update
  53.7 0.0 all-reduce.3.cloned.1.call-start
  53.7 6.6 %split.9 = bf16[64,1,23,2048]{3,2,1,0:T(8,128)(2,1)} slice(bf16[64,1,31,2048]{3,2,1,0:T(8,128)(2,1)} %bitcast.21), slice={[0:64], [0:1], [8:31], [0:2048]} | slice | bytes 12058624 | tf_op jit(solution)/shard_map/split | solution.py:29
  60.3 0.0 all-to-all-done.1
  60.3 123.9 %all_to_all.15 = bf16[64,1,23,2048]{3,2,1,0:T(8,128)(2,1)} all-to-all(bf16[64,1,23,2048]{3,2,1,0:T(8,128)(2,1)} %split.9), channel_id=1, replica_groups=mesh['rep'=4,'exp'=8,'shard'=8] {'exp','shard'}, dimensions={0} | all-to-all | bytes 12058624 | tf_op jit(solution)/shard_map/all_to_all | solution.py:31
  184.2 8.0 %pad_maximum_fusion = bf16[64,1,31,2048]{3,2,1,0:T(8,128)(2,1)} fusion(bf16[64,1,23,2048]{3,2,1,0:T(8,128)(2,1)} %all_to_all.15, bf16[64,1,8,2048]{3,2,1,0:T(8,128)(2,1)S(1)} %all-to-all-done.1), kind=kLoop, calls=%fused_computation | loop fusion | flops 16252928 | bytes 16252928 | tf_op jit(solution)/shard_map/concatenate | solution.py:32
  192.2 9.8 %reshape_reshape.7 = bf16[1984,2048]{1,0:T(8,128)(2,1)} reshape(bf16[64,1,31,2048]{3,2,1,0:T(8,128)(2,1)} %pad_maximum_fusion) | data formatting | bytes 16252928 | tf_op jit(solution)/shard_map/reshape;reshape | solution.py:64
  201.9 13.7 %convert_bitcast_fusion = bf16[1,2048,896]{2,1,0:T(8,128)(2,1)} fusion(bf16[1984,2048]{1,0:T(8,128)(2,1)} %reshape_reshape.7, bf16[1,1984,896]{2,1,0:T(8,128)(2,1)} %param.7), kind=kOutput, calls=%fused_computation.3 | convolution fusion | flops 7283146752 | bytes 15351808 | tf_op jit(solution)/shard_map/dot_general | solution.py:63
  215.7 0.0 all-reduce.3.cloned.1.call-update
  215.7 13.1 %reduce-scatter.2.cloned.1.call-done = bf16[248,2048]{1,0:T(8,128)(2,1)} async-done(((bf16[1984,2048]{1,0:T(8,128)(2,1)}), bf16[248,2048]{1,0:T(8,128)(2,1)}) %reduce-scatter.2.cloned.1.call-update) | async-done | bytes 1015824 | tf_op jit(solution)/shard_map/reduce_scatter | solution.py:68
  228.8 1.5 reshape.52
  230.3 21.5 %all_to_all.16 = bf16[8,31,2048]{2,1,0:T(8,128)(2,1)S(1)} all-to-all(bf16[8,31,2048]{2,1,0:T(8,128)(2,1)S(1)} %reshape.52), channel_id=1, replica_groups=mesh['rep'=4,'exp'=8,'shard'=8] {'exp'}, dimensions={0} | all-to-all | bytes 2031616 | tf_op jit(solution)/shard_map/all_to_all | solution.py:77
  251.9 0.3 reshape.53
  252.2 0.0 copy-start.1
  252.2 1.1 convolution_convert_fusion.2
  253.3 117.9 %all-reduce.3.cloned.1.call-done = bf16[1,2048,896]{2,1,0:T(8,128)(2,1)} async-done(((bf16[1,2048,896]{2,1,0:T(8,128)(2,1)}), bf16[1,2048,896]{2,1,0:T(8,128)(2,1)}) %all-reduce.3.cloned.1.call-update) | async-done | bytes 3670032 | tf_op jit(solution)/shard_map/psum | solution.py:66
  371.2 4.2 %copy.14 = bf16[1,2048,896]{2,1,0:T(8,128)(2,1)} copy(bf16[1,2048,896]{2,1,0:T(8,128)(2,1)} %all-reduce.3.cloned.1.call-done) | data formatting | bytes 7340032
  375.4 0.0 copy-done.1
  (6 shorter events, 0.1 us)
Async XLA Ops:
  8.0 2.3 copy-start
  12.1 3.2 copy-start.2
  16.8 43.5 %all-to-all-start.1 = ((bf16[64,1,8,2048]{3,2,1,0:T(8,128)(2,1)}), bf16[64,1,8,2048]{3,2,1,0:T(8,128)(2,1)S(1)}, u32[]{:S(2)}, u32[]{:S(2)}) async-start(bf16[64,1,8,2048]{3,2,1,0:T(8,128)(2,1)} %split.8), calls=%async_computation.2 | async-start | bytes 4194304 | tf_op jit(solution)/shard_map/all_to_all | solution.py:31
  26.3 202.5 %reduce-scatter.2.cloned.1.call-start = ((), (), s32[]{:S(2)}) async-start(), calls=%async_computation.4 | async-start | bytes 9142272 | tf_op jit(solution)/shard_map/reduce_scatter | solution.py:68
  53.7 317.5 %all-reduce.3.cloned.1.call-start = ((), (), s32[]{:S(2)}) async-start(), calls=%async_computation.5 | async-start | bytes 7340032 | tf_op jit(solution)/shard_map/psum | solution.py:66
  252.2 123.2 %copy-start.1 = (bf16[112,2048]{1,0:T(8,128)(2,1)S(1)}, bf16[112,2048]{1,0:T(8,128)(2,1)}, u32[]{:S(2)}) copy-start(bf16[112,2048]{1,0:T(8,128)(2,1)} %param.4) | copy-start | bytes 1376260
Sparse Core Ops, SparseCore 0:
  53.8 174.9 reduce-scatter.1
Sparse Core Ops, SparseCore 1:
  215.8 155.4 all-reduce.2
where the time goes:
time: 384 us; the launch traced here: 383 us
  blocking collectives  145 us (38%)
  waiting for transfers between devices  131 us (34%)
  local copies, waits for them, and re-layouts  43.7 us (11%)
  matrix products  28.7 us (7%)
  between operations  15.6 us (4%)
  starting transfers between devices  9.51 us (2%)
  other arithmetic  8.88 us (2%)
    all_to_all x1, blocking collectives, cut_exchange(): lax.all_to_all(slab, axis, split_axis=0, concat_axis=0, tiled=True)  124 us
    psum x1, waiting for transfers between devices, body(): weight_grad = lax.psum(partial_grad.astype(jnp.bfloat16), 'rep')[None]  118 us
    all_to_all x1, blocking collectives, body(): lax.all_to_all(slot_grad, 'exp', split_axis=0, concat_axis=0, tiled=True)  21.5 us
    dot_general x1, matrix products, body(): lax.dot_general(arrived.reshape(-1, features), cotangent, contract_rows,...  13.7 us
    dot_general x1, matrix products, body(): lax.dot_general(ordered, weight, (((1,), (1,)), ((), ())), preferred_elem...  13.4 us
    reduce_scatter x1, waiting for transfers between devices, body(): lax.psum_scatter(lax.dot_general(ordered, weight, (((1,), (1,)), ((), ())...  13.1 us
    another operation x1, local copies, waits for them, and re-layouts, body(): arrived.reshape(-1, features)  9.75 us
    all_to_all x1, starting transfers between devices, cut_exchange(): lax.all_to_all(slab, axis, split_axis=0, concat_axis=0, tiled=True)  9.43 us
  transfers between devices with their start and end apart: 3, of which 2 were waited for; matrix products, arithmetic and copies ran while one was open for 18% of the time, Pallas kernels for 0%

commit v1 on v0

v1 whole, which is shorter than its diff:
```python
import functools

import jax
import jax.numpy as jnp
from jax import lax
from jax.experimental import pallas as pl
from jax.experimental.pallas import tpu as pltpu
from jax.sharding import PartitionSpec as P

MESH = pl.DeviceIdType.MESH
BF = jnp.bfloat16
F32 = jnp.float32
CHUNKS = 8
BLOCK = 32


def contract(a, b, da, db):
    return lax.dot_general(a, b, (((da,), (db,)), ((), ())), preferred_element_type=F32)


def kernel(
    sizes, tok, routes, w_hbm, c_hbm, tg_out, wg_out,
    cn, cp, wv, plt, tp, snd, g, prod, rr, u, x2, zs, zo, zr, acc, sb, rb,
    load_sem, pl_sem, t_sem, t_rsem, s_a, r_a, s_b, r_b, s_f, r_f, s_r, r_r, s_m, r_m, s_n, r_n, s_d, r_d, s_g, r_g,
):
    reps, experts, ys, slot_cap, width = sizes
    rep, me, shard = lax.axis_index("rep"), lax.axis_index("exp"), lax.axis_index("shard")
    zl, y = shard // ys, lax.rem(shard, ys)
    y_at = lambda k: lax.rem(y + k + 4 * ys, ys)
    r_at = lambda k: lax.rem(rep + k + 4 * reps, reps)
    y_to = ({"shard": zl * ys + y_at(1)}, {"shard": zl * ys + y_at(-1)})
    r_to = ({"rep": r_at(1)}, {"rep": r_at(-1)})
    z_to = {"shard": (1 - zl) * ys + y}
    exp_to = [{"exp": lax.rem(me + d, experts)} for d in range(1, experts)]
    others = experts - 1
    y_block = lambda k: (y_at(-1 - k), y_at(1 + k))
    r_block = lambda k: (r_at(-1 - k), r_at(1 + k))
    planes = (zl, 1 - zl)

    def rc(src, dst, ssem, rsem, dev):
        return pltpu.make_async_remote_copy(
            src_ref=src, dst_ref=dst, send_sem=ssem, recv_sem=rsem, device_id=dev, device_id_type=MESH
        )

    load_c = pltpu.make_async_copy(c_hbm, cn, load_sem.at[0])
    load_w = pltpu.make_async_copy(w_hbm, wv, load_sem.at[1])
    load_c.start()
    load_w.start()

    barrier = pltpu.get_barrier_semaphore()
    peers = [*y_to, *r_to, z_to, *exp_to]
    for dev in peers:
        pl.semaphore_signal(barrier, inc=1, device_id=dev, device_id_type=MESH)

    rows = tok.shape[0]
    slots = experts * BLOCK
    lane = lax.broadcasted_iota(jnp.int32, (rows, 128), 1)
    named = ((routes[:, 0:1] == lane) | (routes[:, 1:2] == lane)).astype(F32).astype(BF)
    before = (
        lax.broadcasted_iota(jnp.int32, (rows, rows), 1) < lax.broadcasted_iota(jnp.int32, (rows, rows), 0)
    ).astype(F32).astype(BF)
    position = contract(before, named, 1, 0).astype(BF)
    spread = (
        lax.broadcasted_iota(jnp.int32, (128, slots), 0) == lax.broadcasted_iota(jnp.int32, (128, slots), 1) // BLOCK
    ).astype(F32).astype(BF)
    slot_of = lax.rem(lax.broadcasted_iota(jnp.int32, (rows, slots), 1), BLOCK).astype(F32)
    hit = contract(named, spread, 1, 0)
    where = contract(position, spread, 1, 0)
    plt[0] = jnp.where(where == slot_of, hit, 0.0).astype(BF)

    pl.semaphore_wait(barrier, len(peers))

    send_pl = rc(plt.at[0], plt.at[1], pl_sem.at[0], pl_sem.at[1], z_to)
    send_pl.start()
    cols = lambda c: pl.ds(pl.multiple_of(c * width, 128), width)

    def send_tokens(c):
        return rc(tok.at[:, cols(c)], tp.at[:, cols(c)], t_sem.at[c], t_rsem.at[c], z_to)

    @pl.loop(0, CHUNKS)
    def _(c):
        send_tokens(c).start()

    load_c.wait()
    load_w.wait()

    row = lax.broadcasted_iota(jnp.int32, (2 * ys * BLOCK, 2 * ys * slot_cap), 0)
    col = lax.broadcasted_iota(jnp.int32, (2 * ys * BLOCK, 2 * ys * slot_cap), 1)
    inner = lax.rem(row, BLOCK)
    spaced = jnp.where((col == (row // BLOCK) * slot_cap + inner) & (inner < slot_cap), 1.0, 0.0).astype(BF)

    @pl.loop(0, experts)
    def _(e):
        moved = contract(spaced, cn[e], 1, 0).astype(BF)
        for z in range(2):
            for yy in range(ys):
                at = (z * ys + yy) * BLOCK
                cp[yy * 2 + z, e] = moved[at : at + BLOCK]

    slab = slots

    def a_copies(c, p):
        at = y * 2 + planes[p]
        return [
            rc(snd.at[c, p, dev["exp"]], g.at[c, at, me], s_a.at[c % 2, p], r_a.at[c, p], dev) for dev in exp_to
        ]

    def a_all(c, p):
        at = y * 2 + planes[p]
        return rc(g.at[c, at, pl.ds(0, others)], g.at[c, at, pl.ds(0, others)], s_a.at[c % 2, p], r_a.at[c, p], exp_to[0])

    def stage_a(c):
        for p in range(2):
            if p == 1:
                send_tokens(c).wait_recv()

                @pl.when(c == 0)
                def _():
                    send_pl.wait_recv()

            source = (tok, tp)[p][:, cols(c)]
            made = contract(plt[p], source, 0, 0).astype(BF).reshape(experts, BLOCK, width)
            snd[c, p] = made
            g[c, y * 2 + planes[p], me] = snd[c, p, me]
            for copy in a_copies(c, p):
                copy.start()

    def b_copies(c):
        return [
            rc(g.at[c, y * 2 + p], g.at[c, y * 2 + p], s_b.at[c % 2, d, p], r_b.at[c, d, p], y_to[d])
            for p in range(2)
            for d in range(2)
        ]

    def b_arrived(c, d, p):
        at = (y_at(-1), y_at(1))[d] * 2 + p
        return rc(g.at[c, at], g.at[c, at], s_b.at[c % 2, d, p], r_b.at[c, d, p], y_to[d])

    def f_copies(c):
        out = []
        for d in range(2):
            at = (y_at(-1), y_at(1))[d] * 2 + d
            out.append(rc(g.at[c, at], g.at[c, at], s_f.at[c % 2, d], r_f.at[c, d], y_to[d]))
        return out

    def stage_b(c):
        for p in range(2):
            a_all(c, p).wait_recv()
        for copy in b_copies(c):
            copy.start()

    def stage_f(c):
        copies = f_copies(c)
        for d in range(2):
            b_arrived(c, d, d).wait_recv()
            copies[d].start()

    def stage_w(c):
        b_arrived(c, 0, 1).wait_recv()
        b_arrived(c, 1, 0).wait_recv()
        for copy in f_copies(c):
            copy.wait_recv()
        grad = contract(g[c].reshape(2 * ys * slab, width), cp[...].reshape(2 * ys * slab, -1), 0, 0)
        acc[c % 2] = grad.reshape(2 * reps, width // (2 * reps), -1)
        for d in range(2):
            sb[c % 2, d] = acc[c % 2, r_block(0)[d] * 2 + d].astype(BF)
        for copy in d_copies(c, 0):
            copy.start()

    def d_copies(c, k):
        return [
            rc(sb.at[c % 2, d] if k == 0 else rb.at[c, k - 1, d], rb.at[c, k, d], s_d.at[c % 2, k, d], r_d.at[c, k, d], r_to[d])
            for d in range(2)
        ]

    def stage_d(c, k):
        came, send = d_copies(c, k - 1), d_copies(c, k)
        for d in range(2):
            came[d].wait_recv()
            rb[c, k - 1, d] = (rb[c, k - 1, d].astype(F32) + acc[c % 2, r_block(k)[d] * 2 + d]).astype(BF)
            send[d].start()

    def g_copies(c, k):
        out = []
        for d in range(2):
            at = (r_at(-k), r_at(k))[d] * 2 + d
            out.append(rc(wg_out.at[c, at], wg_out.at[c, at], s_g.at[c % 2, k, d], r_g.at[c, k, d], r_to[d]))
        return out

    def stage_e(c):
        came, send = d_copies(c, 2), g_copies(c, 0)
        for d in range(2):
            came[d].wait_recv()
            wg_out[c, rep * 2 + d] = (rb[c, 2, d].astype(F32) + acc[c % 2, rep * 2 + d]).astype(BF)
            send[d].start()

    def stage_g(c, k):
        came, send = g_copies(c, k - 1), g_copies(c, k)
        for d in range(2):
            came[d].wait_recv()
            send[d].start()

    def stage_end(c):
        for copy in g_copies(c, 2):
            copy.wait_recv()

    def r_copies(c, k):
        out = []
        for d in range(2):
            src = prod.at[c % 2, y_block(0)[d] * 2 + d] if k == 0 else rr.at[c, k - 1, d]
            out.append(rc(src, rr.at[c, k, d], s_r.at[c % 2, k, d], r_r.at[c, k, d], y_to[d]))
        return out

    def stage_p(c):
        weights = wv[cols(c), :]

        @pl.loop(0, 2 * ys)
        def _(s):
            prod[c % 2, s] = contract(cp[s].reshape(slab, -1), weights, 1, 1).astype(BF)

        for copy in r_copies(c, 0):
            copy.start()

    def stage_r(c, k):
        came, send = r_copies(c, k - 1), r_copies(c, k)
        for d in range(2):
            came[d].wait_recv()
            rr[c, k - 1, d] = (rr[c, k - 1, d].astype(F32) + prod[c % 2, y_block(k)[d] * 2 + d].astype(F32)).astype(BF)
            send[d].start()

    def m_copies(c, d):
        return [rc(u.at[c, d, dev["exp"]], x2.at[c, d, me], s_m.at[c % 2, d], r_m.at[c, d], dev) for dev in exp_to]

    def m_all(c, d):
        return rc(x2.at[c, d, pl.ds(0, others)], x2.at[c, d, pl.ds(0, others)], s_m.at[c % 2, d], r_m.at[c, d], exp_to[0])

    def stage_m(c):
        came = r_copies(c, 2)
        for d in range(2):
            came[d].wait_recv()
            total = rr[c, 2, d].astype(F32) + prod[c % 2, y * 2 + d].astype(F32)
            u[c, d] = total.astype(BF).reshape(experts, BLOCK, width)
            x2[c, d, me] = u[c, d, me]
            for copy in m_copies(c, d):
                copy.start()

    def n_copy(c):
        return rc(zs.at[c], zr.at[c], s_n.at[c % 2], r_n.at[c], z_to)

    def stage_n(c):
        for d in range(2):
            m_all(c, d).wait_recv()
        theirs = contract(plt[1], x2[c, planes[1]].reshape(slots, width), 1, 0)
        zs[c] = theirs.astype(BF)
        n_copy(c).start()
        zo[c] = contract(plt[0], x2[c, planes[0]].reshape(slots, width), 1, 0)

    def stage_o(c):
        n_copy(c).wait_recv()
        tg_out[:, cols(c)] = (zo[c] + zr[c].astype(F32)).astype(BF)

    def at(t, offset, stage):
        c = t - offset

        @pl.when((c >= 0) & (c < CHUNKS))
        def _():
            stage(c)

    def wait_sends(make):
        def stage(c):
            for copy in make(c):
                copy.wait_send()

        return stage

    first = 1

    @pl.loop(0, CHUNKS + first + 4)
    def _(t):
        at(t, first, stage_p)
        at(t, 1, stage_b)
        at(t, 0, stage_a)
        at(t, 2, stage_w)
        at(t, first + 1, stage_m)
        at(t, 3, stage_e)
        at(t, first + 2, stage_n)
        at(t, first + 3, stage_o)

        at(t, first, functools.partial(stage_r, k=1))
        at(t, 1, stage_f)
        at(t, 2, functools.partial(stage_d, k=1))
        at(t, 3, functools.partial(stage_g, k=1))
        at(t, 1, wait_sends(lambda c: [a_all(c, 0), a_all(c, 1)]))
        at(t, 2, wait_sends(lambda c: b_copies(c) + f_copies(c)))
        at(t, 3, wait_sends(lambda c: d_copies(c, 0) + d_copies(c, 1) + d_copies(c, 2)))
        at(t, 4, wait_sends(lambda c: g_copies(c, 0) + g_copies(c, 1) + g_copies(c, 2)))
        at(t, first + 1, wait_sends(lambda c: r_copies(c, 0) + r_copies(c, 1) + r_copies(c, 2)))
        at(t, first + 2, wait_sends(lambda c: [m_all(c, 0), m_all(c, 1)]))
        at(t, first + 3, wait_sends(lambda c: [n_copy(c), send_tokens(c)]))

        at(t, first, functools.partial(stage_r, k=2))
        at(t, 2, functools.partial(stage_d, k=2))
        at(t, 3, functools.partial(stage_g, k=2))
        at(t, 4, stage_end)

    send_pl.wait_send()


def solution(mesh):
    reps, experts, shards = (mesh.shape[a] for a in ("rep", "exp", "shard"))
    ys = shards // 2

    def body(tokens, routes, gate_weight, gate_cotangent):
        rows, features = tokens.shape
        hidden = gate_weight.shape[2]
        slot_cap = gate_cotangent.shape[1] // (experts * shards)
        width = features // CHUNKS
        n = CHUNKS
        slots = experts * BLOCK
        cotangent = gate_cotangent.reshape(experts, shards * slot_cap, hidden)
        vmem = lambda *shape: pltpu.VMEM(shape, BF)
        wide = lambda *shape: pltpu.VMEM(shape, F32)
        dma = lambda *shape: pltpu.SemaphoreType.DMA(shape)
        whole = pl.BlockSpec(memory_space=pltpu.VMEM)
        far = pl.BlockSpec(memory_space=pl.ANY)
        piece = width // (2 * reps)
        scratch = [
            vmem(experts, shards * slot_cap, hidden),
            vmem(shards, experts, BLOCK, hidden),
            vmem(features, hidden),
            vmem(2, rows, slots),
            vmem(rows, features),
            vmem(n, 2, experts, BLOCK, width),
            vmem(n, shards, experts, BLOCK, width),
            vmem(2, shards, slots, width),
            vmem(n, 3, 2, slots, width),
            vmem(n, 2, experts, BLOCK, width),
            vmem(n, 2, experts, BLOCK, width),
            vmem(n, rows, width),
            wide(n, rows, width),
            vmem(n, rows, width),
            wide(2, 2 * reps, piece, hidden),
            vmem(2, 2, piece, hidden),
            vmem(n, 3, 2, piece, hidden),
            dma(2), dma(2), dma(n), dma(n),
            dma(2, 2), dma(n, 2),
            dma(2, 2, 2), dma(n, 2, 2),
            dma(2, 2), dma(n, 2),
            dma(2, 3, 2), dma(n, 3, 2),
            dma(2, 2), dma(n, 2),
            dma(2), dma(n),
            dma(2, 3, 2), dma(n, 3, 2),
            dma(2, 3, 2), dma(n, 3, 2),
        ]
        token_grad, weight_grad = pl.pallas_call(
            functools.partial(kernel, (reps, experts, ys, slot_cap, width)),
            out_shape=(
                jax.ShapeDtypeStruct((rows, features), BF),
                jax.ShapeDtypeStruct((n, 2 * reps, piece, hidden), BF),
            ),
            in_specs=[whole, whole, far, far],
            out_specs=(whole, whole),
            scratch_shapes=scratch,
            compiler_params=pltpu.CompilerParams(
                collective_id=0, has_side_effects=True, vmem_limit_bytes=67_000_000
            ),
            name="moe_gate_backward",
        )(tokens, routes, gate_weight[0], cotangent)
        return token_grad, weight_grad.reshape(1, features, hidden)

    spec = P(("rep", "exp", "shard"), None)
    return jax.shard_map(
        body,
        mesh=mesh,
        in_specs=(spec, spec, P("exp", None, "shard"), P("exp", "rep", "shard")),
        out_specs=(spec, P("exp", None, "shard")),
        check_vma=False,
    )
```

time: 384 us -> 211 us (0.55)
  the two profiles are of different devices: /device:TPU:39 before, /device:TPU:12 now
where the time goes in v1:
time: 211 us
  Pallas kernels  203 us (96%)
  local copies, waits for them, and re-layouts  7.39 us (4%)
    pallas_call x1, Pallas kernels, body(): pl.pallas_call(functools.partial(kernel, (reps, experts, ys, slot_cap, wi...  203 us
    unnamed x3, local copies, waits for them, and re-layouts  7.39 us

profile of v1, /device:TPU:12, one launch (start us, length us, event | category | flops | bytes accessed | tf_op | source)
XLA Modules:
  0.0 210.8 jit_solution(15939570889982225992)
XLA Ops:
  0.6 1.4 copy.6.routes
  2.0 202.7 %moe_gate_backward.1 = (bf16[112,2048]{1,0:T(8,128)(2,1)}, bf16[8,8,32,896]{3,2,1,0:T(8,128)(2,1)}) custom-call(bf16[112,2048]{1,0:T(8,128)(2,1)} %tok.1, s32[112,2]{1,0:T(8,128)} %copy.6.routes, bf16[2048,896]{1,0:T(8,128)(2,1)} %bitcast.3, bf16[8,248,896]{2,1,0:T(8,128)(2,1)} %bitcast.5), custom_call_target="tpu_custom_call" | custom-call | tf_op jit(solution)/shard_map/moe_gate_backward/pallas_call | solution.py:355
  204.8 1.8 copy.9
  206.6 4.2 %copy.10 = bf16[1,2048,896]{2,1,0:T(8,128)(2,1)} copy(bf16[1,2048,896]{2,1,0:T(8,128)(2,1)} %bitcast.4) | data formatting | bytes 7340032

commit v2 on v1

v2 whole, which is shorter than its diff:
```python
import functools

import jax
import jax.numpy as jnp
from jax import lax
from jax.experimental import pallas as pl
from jax.experimental.pallas import tpu as pltpu
from jax.sharding import PartitionSpec as P

MESH = pl.DeviceIdType.MESH
BF = jnp.bfloat16
F32 = jnp.float32
CHUNKS = 16
EARLY = 3
KEEP = 8
VMEM = 50_000_000
BLOCK = 32


def contract(a, b, da, db):
    return lax.dot_general(a, b, (((da,), (db,)), ((), ())), preferred_element_type=F32)


def kernel(
    sizes, tok_hbm, routes_hbm, c_hbm, w_hbm, tg_out, wg_out,
    tok, routes, cn, cp, wv, pls, tp, snd, g, prod, rr, rr1, u, x2, zs, zo, zr, acc, sb, rb, rc1,
    load_sem, pl_sem, t_sem, t_rsem, s_z, r_z, s_a, r_a, s_b, r_b, s_f, r_f, s_r, r_r, s_m, r_m, s_n, r_n, s_d, r_d, s_g, r_g,
):
    reps, experts, ys, slot_cap, width = sizes
    rep, me, shard = lax.axis_index("rep"), lax.axis_index("exp"), lax.axis_index("shard")
    zl, y = shard // ys, lax.rem(shard, ys)
    y_at = lambda k: lax.rem(y + k + 4 * ys, ys)
    swap = lambda i: (i + 1 - 2 * lax.rem(i, 2), 3 - i)
    bits = lambda i: (lax.rem((i + 1) // 2, 2), i // 2)
    y_pair, r_pair = swap(y), swap(rep)
    y_far = lax.rem(y + 2, ys)
    r_bit = bits(rep)
    y_to = ({"shard": zl * ys + y_at(1)}, {"shard": zl * ys + y_at(-1)})
    y_by = tuple({"shard": zl * ys + i} for i in y_pair)
    r_by = tuple({"rep": i} for i in r_pair)
    z_to = {"shard": (1 - zl) * ys + y}
    exp_to = [{"exp": lax.rem(me + d, experts)} for d in range(1, experts)]
    others = experts - 1
    planes = (zl, 1 - zl)

    def rc(src, dst, ssem, rsem, dev):
        return pltpu.make_async_remote_copy(
            src_ref=src, dst_ref=dst, send_sem=ssem, recv_sem=rsem, device_id=dev, device_id_type=MESH
        )

    loads = [
        pltpu.make_async_copy(src, dst, load_sem.at[i])
        for i, (src, dst) in enumerate(((routes_hbm, routes), (tok_hbm, tok), (c_hbm, cn), (w_hbm, wv)))
    ]
    for load in loads:
        load.start()

    barrier = pltpu.get_barrier_semaphore()
    cross_to = [{**dev, **z_to} for dev in exp_to]
    peers = [*y_to, *r_by, z_to, *exp_to, *cross_to]
    for dev in peers:
        pl.semaphore_signal(barrier, inc=1, device_id=dev, device_id_type=MESH)

    loads[0].wait()
    rows = tok.shape[0]
    slots = experts * BLOCK
    name = lax.broadcasted_iota(jnp.int32, (experts, rows), 0)
    named = ((routes[0:1, :] == name) | (routes[1:2, :] == name)).astype(F32).astype(BF)
    before = (
        lax.broadcasted_iota(jnp.int32, (rows, rows), 0) < lax.broadcasted_iota(jnp.int32, (rows, rows), 1)
    ).astype(F32).astype(BF)
    position = contract(named, before, 1, 0).astype(BF)
    spread = (
        lax.broadcasted_iota(jnp.int32, (slots, experts), 0) // BLOCK
        == lax.broadcasted_iota(jnp.int32, (slots, experts), 1)
    ).astype(F32).astype(BF)
    slot_of = lax.rem(lax.broadcasted_iota(jnp.int32, (slots, rows), 0), BLOCK).astype(F32)
    hit = contract(spread, named, 1, 0)
    where = contract(spread, position, 1, 0)
    pls[0] = jnp.where(where == slot_of, hit, 0.0).astype(BF)

    pl.semaphore_wait(barrier, len(peers))

    send_pl = rc(pls.at[0], pls.at[1], pl_sem.at[0], pl_sem.at[1], z_to)
    loads[1].wait()
    cols = lambda c: pl.ds(pl.multiple_of(c * width, 128), width)

    def send_tokens(c):
        return rc(tok.at[:, cols(c)], tp.at[:, cols(c)], t_sem.at[c], t_rsem.at[c], z_to)

    slab = slots

    def a_copies(c, p):
        at = y * 2 + planes[p]
        return [
            rc(snd.at[c % 4, p, dev["exp"]], g.at[c, at, me], s_a.at[c % 4, p], r_a.at[c, p], dev) for dev in exp_to
        ]

    def a_all(c, p):
        at = y * 2 + planes[p]
        return rc(g.at[c, at, pl.ds(0, others)], g.at[c, at, pl.ds(0, others)], s_a.at[c % 4, p], r_a.at[c, p], exp_to[0])

    def pair_copy(c, slot):
        return rc(snd.at[slot, 0, me], g.at[c, y * 2 + zl, me], s_z.at[c], r_z.at[c], z_to)

    def pair_came(c):
        block = g.at[c, y * 2 + 1 - zl, me]
        return rc(block, block, s_z.at[c], r_z.at[c], z_to)

    def early_a(c):
        snd[c, 0] = contract(pls[0], tok[:, cols(c)], 1, 0).astype(BF).reshape(experts, BLOCK, width)
        g[c, y * 2 + zl, me] = snd[c, 0, me]
        for copy in a_copies(c, 0):
            copy.start()
        for dev in cross_to:
            rc(snd.at[c, 0, dev["exp"]], g.at[c, y * 2 + zl, me], s_a.at[c, 1], r_a.at[c, 1], dev).start()
        pair_copy(c, c).start()

    def stage_a(c, p):
        if p == 1:
            send_tokens(c).wait_recv()

            @pl.when(c == EARLY)
            def _():
                send_pl.wait_recv()

        source = (tok, tp)[p][:, cols(c)]
        made = contract(pls[p], source, 1, 0).astype(BF).reshape(experts, BLOCK, width)
        snd[c % 4, p] = made
        g[c, y * 2 + planes[p], me] = snd[c % 4, p, me]
        for copy in a_copies(c, p):
            copy.start()

    def early_only(c, do):
        if isinstance(c, int):
            do()
        else:
            pl.when(c < EARLY)(do)

    def b_copies(c):
        return [
            rc(g.at[c, y * 2 + p], g.at[c, y * 2 + p], s_b.at[c % 2, d, p], r_b.at[c, d, p], y_to[d])
            for d, p in ((0, 0), (1, 1), (0, 1), (1, 0))
        ]

    def b_arrived(c, d, p):
        at = (y_at(-1), y_at(1))[d] * 2 + p
        return rc(g.at[c, at], g.at[c, at], s_b.at[c % 2, d, p], r_b.at[c, d, p], y_to[d])

    def f_copies(c):
        out = []
        for d in range(2):
            at = (y_at(-1), y_at(1))[d] * 2 + d
            out.append(rc(g.at[c, at], g.at[c, at], s_f.at[c % 2, d], r_f.at[c, d], y_to[d]))
        return out

    def stage_b(c):
        for p in range(2):
            a_all(c, p).wait_recv()
        early_only(c, lambda: pair_came(c).wait_recv())
        for copy in b_copies(c):
            copy.start()

    def stage_f(c):
        copies = f_copies(c)
        for d in range(2):
            b_arrived(c, d, d).wait_recv()
            copies[d].start()

    def stage_w(c):
        b_arrived(c, 0, 1).wait_recv()
        b_arrived(c, 1, 0).wait_recv()
        for copy in f_copies(c):
            copy.wait_recv()
        grad = contract(g[c].reshape(2 * ys * slab, width), cp[...].reshape(2 * ys * slab, -1), 0, 0)
        acc[c % 4] = grad.reshape(2, 2, 2, width // 8, -1)
        for v in range(2):
            sb[c % 4, v] = acc[c % 4, v, 1 - r_bit[v]].astype(BF)
        for copy in d0_copies(c):
            copy.start()

    def d0_copies(c):
        return [rc(sb.at[c % 4, v], rb.at[c, v], s_d.at[c % 2, 0, v], r_d.at[c, 0, v], r_by[v]) for v in range(2)]

    def d1_copies(c):
        return [
            rc(rb.at[c, v, 1 - r_bit[1 - v]], rc1.at[c, v], s_d.at[c % 2, 1, v], r_d.at[c, 1, v], r_by[1 - v])
            for v in range(2)
        ]

    def stage_d(c):
        came, send = d0_copies(c), d1_copies(c)
        for v in range(2):
            came[v].wait_recv()
            q = 1 - r_bit[1 - v]
            rb[c, v, q] = (rb[c, v, q].astype(F32) + acc[c % 4, v, r_bit[v], q]).astype(BF)
            send[v].start()

    def g0_copies(c):
        out = []
        for v in range(2):
            piece = wg_out.at[c, v, r_bit[v], r_bit[1 - v]]
            out.append(rc(piece, piece, s_g.at[c % 2, 0, v], r_g.at[c, 0, v], r_by[1 - v]))
        return out

    def g1_copies(c):
        out = []
        for v in range(2):
            half = wg_out.at[c, v, r_bit[v]]
            out.append(rc(half, half, s_g.at[c % 2, 1, v], r_g.at[c, 1, v], r_by[v]))
        return out

    def stage_e(c):
        came, send = d1_copies(c), g0_copies(c)
        for v in range(2):
            came[v].wait_recv()
            h, q = r_bit[v], r_bit[1 - v]
            total = acc[c % 4, v, h, q] + rb[c, v, q].astype(F32) + rc1[c, v].astype(F32)
            wg_out[c, v, h, q] = total.astype(BF)
            send[v].start()

    def stage_g(c):
        came, send = g0_copies(c), g1_copies(c)
        for v in range(2):
            came[v].wait_recv()
            send[v].start()

    def stage_end(c):
        for copy in g1_copies(c):
            copy.wait_recv()

    def r0_copies(c):
        return [
            rc(prod.at[c % KEEP, (y_pair[v], y_far)[i] * 2 + v], rr.at[c, v, i], s_r.at[c % 2, i, v], r_r.at[c, i, v], y_by[v])
            for i in (1, 0)
            for v in range(2)
        ]

    def r1_copies(c):
        return [rc(rr.at[c, v, 1], rr1.at[c, v], s_r.at[c % 2, 2, v], r_r.at[c, 2, v], y_by[1 - v]) for v in range(2)]

    def stage_p(c):
        odd = lax.rem(c, 2)
        pair = c - odd
        weights = wv[pl.ds(pl.multiple_of(pair * width, 256), 2 * width), :]

        @pl.loop(0, ys)
        def _(i):
            s = odd * ys + i
            made = contract(cp[s].reshape(slab, -1), weights, 1, 1).astype(BF)
            for j in range(2):
                prod[lax.rem(pair + j, KEEP), s] = made[:, j * width : (j + 1) * width]

    def stage_r0(c):
        for copy in r0_copies(c):
            copy.start()

    def stage_r1(c):
        came, send = r0_copies(c), r1_copies(c)
        for v in range(2):
            came[v].wait_recv()
            mine = prod[c % KEEP, y_pair[1 - v] * 2 + v].astype(F32)
            rr[c, v, 1] = (rr[c, v, 1].astype(F32) + mine).astype(BF)
            send[v].start()

    def m_copies(c, d):
        return [rc(u.at[c % 4, d, dev["exp"]], x2.at[c, d, me], s_m.at[c % 2, d], r_m.at[c, d], dev) for dev in exp_to]

    def m_all(c, d):
        return rc(x2.at[c, d, pl.ds(0, others)], x2.at[c, d, pl.ds(0, others)], s_m.at[c % 2, d], r_m.at[c, d], exp_to[0])

    def stage_m(c):
        first_half, second = r0_copies(c), r1_copies(c)
        for d in range(2):
            first_half[2 + d].wait_recv()
            second[d].wait_recv()
            total = rr[c, d, 0].astype(F32) + prod[c % KEEP, y * 2 + d].astype(F32) + rr1[c, d].astype(F32)
            u[c % 4, d] = total.astype(BF).reshape(experts, BLOCK, width)
            x2[c, d, me] = u[c % 4, d, me]
            for copy in m_copies(c, d):
                copy.start()

    def n_copy(c):
        return rc(zs.at[c], zr.at[c], s_n.at[c % 2], r_n.at[c], z_to)

    def stage_n(c):
        for d in range(2):
            m_all(c, d).wait_recv()
        theirs = contract(pls[1], x2[c, planes[1]].reshape(slots, width), 0, 0)
        zs[c] = theirs.astype(BF)
        n_copy(c).start()
        zo[c] = contract(pls[0], x2[c, planes[0]].reshape(slots, width), 0, 0)

    def stage_o(c):
        n_copy(c).wait_recv()
        tg_out[:, cols(c)] = (zo[c] + zr[c].astype(F32)).astype(BF)

    def at(t, offset, stage):
        c = t - offset

        @pl.when((c >= 0) & (c < CHUNKS))
        def _():
            stage(c)

    def wait_sends(make):
        def stage(c):
            for copy in make(c):
                copy.wait_send()

        return stage

    def prepare():
        loads[2].wait()
        row = lax.broadcasted_iota(jnp.int32, (2 * ys * BLOCK, 2 * ys * slot_cap), 0)
        col = lax.broadcasted_iota(jnp.int32, (2 * ys * BLOCK, 2 * ys * slot_cap), 1)
        inner = lax.rem(row, BLOCK)
        spaced = jnp.where((col == (row // BLOCK) * slot_cap + inner) & (inner < slot_cap), 1.0, 0.0).astype(BF)

        @pl.loop(0, experts)
        def _(e):
            moved = contract(spaced, cn[e], 1, 0).astype(BF)
            for z in range(2):
                for yy in range(ys):
                    at = (z * ys + yy) * BLOCK
                    cp[yy * 2 + z, e] = moved[at : at + BLOCK]

    first = 3
    ticks = CHUNKS + max(first + 5, 7)

    early_a(0)
    send_pl.start()
    for c in range(1, EARLY):
        early_a(c)

    @pl.loop(EARLY, CHUNKS)
    def _(c):
        send_tokens(c).start()

    prepare()
    loads[3].wait()
    stage_b(0)
    a_all(0, 0).wait_send()
    a_all(0, 1).wait_send()
    pair_copy(0, 0).wait_send()

    @pl.loop(1, ticks)
    def _(t):
        at(t, 6, stage_end)
        at(t, first + 2, stage_m)
        at(t, 5, stage_g)
        at(t, first + 1, stage_r1)
        at(t, 4, stage_e)
        at(t, 1, stage_f)
        at(t, 3, stage_d)
        at(t, first, stage_r0)
        at(t, 0, stage_b)
        at(t, 2, stage_w)
        at(t, first + 3, stage_n)
        at(t, first + 4, stage_o)
        at(t, -2, functools.partial(stage_a, p=0))
        at(t, -2, functools.partial(stage_a, p=1))
        at(t, 0, wait_sends(lambda c: [a_all(c, 0), a_all(c, 1)]))
        at(t, 0, lambda c: early_only(c, lambda: pair_copy(c, c % 4).wait_send()))
        at(t, 1, wait_sends(lambda c: b_copies(c)))
        at(t, 2, wait_sends(lambda c: f_copies(c)))
        at(t, 3, wait_sends(lambda c: d0_copies(c)))
        at(t, 4, wait_sends(lambda c: d1_copies(c)))
        at(t, 5, wait_sends(lambda c: g0_copies(c)))
        at(t, 6, wait_sends(lambda c: g1_copies(c)))
        at(t, first + 1, wait_sends(lambda c: r0_copies(c)))
        at(t, first + 2, wait_sends(lambda c: r1_copies(c)))
        at(t, first + 3, wait_sends(lambda c: [m_all(c, 0), m_all(c, 1)]))
        at(t, first + 4, wait_sends(lambda c: [n_copy(c)]))
        at(t, first + 4, lambda c: pl.when(c >= EARLY)(lambda: send_tokens(c).wait_send()))
        at(t, first - 2, stage_p)

    send_pl.wait_send()


def solution(mesh):
    reps, experts, shards = (mesh.shape[a] for a in ("rep", "exp", "shard"))
    ys = shards // 2

    def body(tokens, routes, gate_weight, gate_cotangent):
        rows, features = tokens.shape
        hidden = gate_weight.shape[2]
        slot_cap = gate_cotangent.shape[1] // (experts * shards)
        width = features // CHUNKS
        n = CHUNKS
        slots = experts * BLOCK
        cotangent = gate_cotangent.reshape(experts, shards * slot_cap, hidden)
        vmem = lambda *shape: pltpu.VMEM(shape, BF)
        wide = lambda *shape: pltpu.VMEM(shape, F32)
        dma = lambda *shape: pltpu.SemaphoreType.DMA(shape)
        whole = pl.BlockSpec(memory_space=pltpu.VMEM)
        far = pl.BlockSpec(memory_space=pltpu.HBM)
        piece = width // 8
        scratch = [
            vmem(rows, features),
            pltpu.VMEM((2, rows), jnp.int32),
            vmem(experts, shards * slot_cap, hidden),
            vmem(shards, experts, BLOCK, hidden),
            vmem(features, hidden),
            vmem(2, slots, rows),
            vmem(rows, features),
            vmem(4, 2, experts, BLOCK, width),
            vmem(n, shards, experts, BLOCK, width),
            vmem(KEEP, shards, slots, width),
            vmem(n, 2, 2, slots, width),
            vmem(n, 2, slots, width),
            vmem(4, 2, experts, BLOCK, width),
            vmem(n, 2, experts, BLOCK, width),
            vmem(n, rows, width),
            wide(n, rows, width),
            vmem(n, rows, width),
            wide(4, 2, 2, 2, piece, hidden),
            vmem(4, 2, 2, piece, hidden),
            vmem(n, 2, 2, piece, hidden),
            vmem(n, 2, piece, hidden),
            dma(4), dma(2), dma(n), dma(n), dma(EARLY), dma(EARLY),
            dma(4, 2), dma(n, 2),
            dma(2, 2, 2), dma(n, 2, 2),
            dma(2, 2), dma(n, 2),
            dma(2, 3, 2), dma(n, 3, 2),
            dma(2, 2), dma(n, 2),
            dma(2), dma(n),
            dma(2, 2, 2), dma(n, 2, 2),
            dma(2, 2, 2), dma(n, 2, 2),
        ]
        token_grad, weight_grad = pl.pallas_call(
            functools.partial(kernel, (reps, experts, ys, slot_cap, width)),
            out_shape=(
                jax.ShapeDtypeStruct((rows, features), BF),
                jax.ShapeDtypeStruct((n, 2, 2, 2, piece, hidden), BF),
            ),
            in_specs=[far, far, far, far],
            out_specs=(whole, whole),
            scratch_shapes=scratch,
            compiler_params=pltpu.CompilerParams(
                collective_id=0, has_side_effects=True, vmem_limit_bytes=VMEM
            ),
            name="moe_gate_backward",
        )(*(pltpu.with_memory_space_constraint(a, pltpu.HBM) for a in (tokens, routes.T, cotangent, gate_weight[0])))
        return token_grad, weight_grad.reshape(1, features, hidden)

    spec = P(("rep", "exp", "shard"), None)
    return jax.shard_map(
        body,
        mesh=mesh,
        in_specs=(spec, spec, P("exp", None, "shard"), P("exp", "rep", "shard")),
        out_specs=(spec, P("exp", None, "shard")),
        check_vma=False,
    )
```

time: 211 us -> 178 us (0.84)
  the two profiles are of different devices: /device:TPU:12 before, /device:TPU:39 now
where the time goes in v2:
time: 178 us; the launch traced here: 175 us
  Pallas kernels  172 us (97%)
  local copies, waits for them, and re-layouts  2.61 us (1%)
    pallas_call x1, Pallas kernels, body(): pl.pallas_call(functools.partial(kernel, (reps, experts, ys, slot_cap, wi...  172 us

profile of v2, /device:TPU:39, one launch (start us, length us, event | category | flops | bytes accessed | tf_op | source)
XLA Modules:
  0.0 174.9 jit_solution(899568088701156438)
XLA Ops:
  0.6 171.6 %moe_gate_backward.1 = (bf16[112,2048]{1,0:T(8,128)(2,1)S(1)}, bf16[16,2,2,2,16,896]{5,4,3,2,1,0:T(8,128)(2,1)S(1)}) custom-call(bf16[112,2048]{1,0:T(8,128)(2,1)} %tok_hbm.1, s32[2,112]{1,0:T(2,128)} %bitcast.7, bf16[8,248,896]{2,1,0:T(8,128)(2,1)} %bitcast.6, bf16[2048,896]{1,0:T(8,128)(2,1)} %bitcast.5), custom_call_target="tpu_custom_call" | custom-call | tf_op jit(solution)/shard_map/moe_gate_backward/pallas_call | solution.py:430
  172.3 0.8 copy.8
  173.1 1.8 %copy.9 = bf16[1,2048,896]{2,1,0:T(8,128)(2,1)} copy(bf16[1,2048,896]{2,1,0:T(8,128)(2,1)S(1)} %bitcast.4) | data formatting | bytes 7340032

commit v3 on v2

--- a/solution.py
+++ b/solution.py
@@ -345,7 +345,6 @@
 
     @pl.loop(1, ticks)
     def _(t):
-        at(t, 6, stage_end)
         at(t, first + 2, stage_m)
         at(t, 5, stage_g)
         at(t, first + 1, stage_r1)
@@ -354,9 +353,10 @@
         at(t, 3, stage_d)
         at(t, first, stage_r0)
         at(t, 0, stage_b)
+        at(t, first + 3, stage_n)
         at(t, 2, stage_w)
-        at(t, first + 3, stage_n)
         at(t, first + 4, stage_o)
+        at(t, 6, stage_end)
         at(t, -2, functools.partial(stage_a, p=0))
         at(t, -2, functools.partial(stage_a, p=1))
         at(t, 0, wait_sends(lambda c: [a_all(c, 0), a_all(c, 1)]))

time: 178 us -> 176 us (0.989)
  Pallas kernels: 172 us -> 169 us
    pallas_call x1, Pallas kernels: 172 us -> 169 us  [body(): pl.pallas_call(functools.partial(kernel, (reps, experts, ys, slot_cap, wi...]
where the time goes in v3:
time: 176 us; the launch traced here: 172 us
  Pallas kernels  169 us (96%)
  local copies, waits for them, and re-layouts  2.61 us (1%)
    pallas_call x1, Pallas kernels, body(): pl.pallas_call(functools.partial(kernel, (reps, experts, ys, slot_cap, wi...  169 us

profile of v3, /device:TPU:39, one launch (start us, length us, event | category | flops | bytes accessed | tf_op | source)
XLA Modules:
  0.0 172.5 jit_solution(2991913122654848067)
XLA Ops:
  0.6 169.2 %moe_gate_backward.1 = (bf16[112,2048]{1,0:T(8,128)(2,1)S(1)}, bf16[16,2,2,2,16,896]{5,4,3,2,1,0:T(8,128)(2,1)S(1)}) custom-call(bf16[112,2048]{1,0:T(8,128)(2,1)} %tok_hbm.1, s32[2,112]{1,0:T(2,128)} %bitcast.7, bf16[8,248,896]{2,1,0:T(8,128)(2,1)} %bitcast.6, bf16[2048,896]{1,0:T(8,128)(2,1)} %bitcast.5), custom_call_target="tpu_custom_call" | custom-call | tf_op jit(solution)/shard_map/moe_gate_backward/pallas_call | solution.py:430
  169.9 0.8 copy.8
  170.6 1.8 %copy.9 = bf16[1,2048,896]{2,1,0:T(8,128)(2,1)} copy(bf16[1,2048,896]{2,1,0:T(8,128)(2,1)S(1)} %bitcast.4) | data formatting | bytes 7340032

commit v4 on v3

--- a/solution.py
+++ b/solution.py
@@ -180,7 +180,12 @@
             copy.start()
 
     def d0_copies(c):
-        return [rc(sb.at[c % 4, v], rb.at[c, v], s_d.at[c % 2, 0, v], r_d.at[c, 0, v], r_by[v]) for v in range(2)]
+        out = []
+        for i in range(2):
+            for v in range(2):
+                q = (1 - r_bit[1 - v], r_bit[1 - v])[i]
+                out.append(rc(sb.at[c % 4, v, q], rb.at[c, v, q], s_d.at[c % 2, 2 * i, v], r_d.at[c, 2 * i, v], r_by[v]))
+        return out
 
     def d1_copies(c):
         return [
@@ -203,21 +208,31 @@
             out.append(rc(piece, piece, s_g.at[c % 2, 0, v], r_g.at[c, 0, v], r_by[1 - v]))
         return out
 
+    def own_copies(c):
+        out = []
+        for v in range(2):
+            piece = wg_out.at[c, v, r_bit[v], r_bit[1 - v]]
+            out.append(rc(piece, piece, s_g.at[c % 2, 2, v], r_g.at[c, 2, v], r_by[v]))
+        return out
+
     def g1_copies(c):
         out = []
         for v in range(2):
-            half = wg_out.at[c, v, r_bit[v]]
-            out.append(rc(half, half, s_g.at[c % 2, 1, v], r_g.at[c, 1, v], r_by[v]))
+            piece = wg_out.at[c, v, r_bit[v], 1 - r_bit[1 - v]]
+            out.append(rc(piece, piece, s_g.at[c % 2, 1, v], r_g.at[c, 1, v], r_by[v]))
         return out
 
     def stage_e(c):
-        came, send = d1_copies(c), g0_copies(c)
-        for v in range(2):
+        came, rest, send, own = d1_copies(c), d0_copies(c), g0_copies(c), own_copies(c)
+        for v in range(2):
+            rest[2 + v].wait_recv()
             came[v].wait_recv()
             h, q = r_bit[v], r_bit[1 - v]
             total = acc[c % 4, v, h, q] + rb[c, v, q].astype(F32) + rc1[c, v].astype(F32)
             wg_out[c, v, h, q] = total.astype(BF)
             send[v].start()
+        for copy in own:
+            copy.start()
 
     def stage_g(c):
         came, send = g0_copies(c), g1_copies(c)
@@ -226,7 +241,7 @@
             send[v].start()
 
     def stage_end(c):
-        for copy in g1_copies(c):
+        for copy in own_copies(c) + g1_copies(c):
             copy.wait_recv()
 
     def r0_copies(c):
@@ -365,7 +380,7 @@
         at(t, 2, wait_sends(lambda c: f_copies(c)))
         at(t, 3, wait_sends(lambda c: d0_copies(c)))
         at(t, 4, wait_sends(lambda c: d1_copies(c)))
-        at(t, 5, wait_sends(lambda c: g0_copies(c)))
+        at(t, 5, wait_sends(lambda c: g0_copies(c) + own_copies(c)))
         at(t, 6, wait_sends(lambda c: g1_copies(c)))
         at(t, first + 1, wait_sends(lambda c: r0_copies(c)))
         at(t, first + 2, wait_sends(lambda c: r1_copies(c)))
@@ -424,8 +439,8 @@
             dma(2, 3, 2), dma(n, 3, 2),
             dma(2, 2), dma(n, 2),
             dma(2), dma(n),
-            dma(2, 2, 2), dma(n, 2, 2),
-            dma(2, 2, 2), dma(n, 2, 2),
+            dma(2, 3, 2), dma(n, 3, 2),
+            dma(2, 3, 2), dma(n, 3, 2),
         ]
         token_grad, weight_grad = pl.pallas_call(
             functools.partial(kernel, (reps, experts, ys, slot_cap, width)),

time: 176 us -> 176 us (level)
  no operation moved by 1% of the time
where the time goes in v4:
time: 176 us; the launch traced here: 173 us
  Pallas kernels  169 us (96%)
  local copies, waits for them, and re-layouts  2.61 us (1%)
    pallas_call x1, Pallas kernels, body(): pl.pallas_call(functools.partial(kernel, (reps, experts, ys, slot_cap, wi...  169 us

profile of v4, /device:TPU:39, one launch (start us, length us, event | category | flops | bytes accessed | tf_op | source)
XLA Modules:
  0.0 172.7 jit_solution(9259835856345780073)
XLA Ops:
  0.6 169.4 %moe_gate_backward.1 = (bf16[112,2048]{1,0:T(8,128)(2,1)S(1)}, bf16[16,2,2,2,16,896]{5,4,3,2,1,0:T(8,128)(2,1)S(1)}) custom-call(bf16[112,2048]{1,0:T(8,128)(2,1)} %tok_hbm.1, s32[2,112]{1,0:T(2,128)} %bitcast.7, bf16[8,248,896]{2,1,0:T(8,128)(2,1)} %bitcast.6, bf16[2048,896]{1,0:T(8,128)(2,1)} %bitcast.5), custom_call_target="tpu_custom_call" | custom-call | tf_op jit(solution)/shard_map/moe_gate_backward/pallas_call | solution.py:445
  170.1 0.8 copy.8
  170.8 1.8 %copy.9 = bf16[1,2048,896]{2,1,0:T(8,128)(2,1)} copy(bf16[1,2048,896]{2,1,0:T(8,128)(2,1)S(1)} %bitcast.4) | data formatting | bytes 7340032
